TPU v7x, 32 devices: a whole 2x2x4 slice. The times are simulated.
32 devices in a mesh: owner: 8 (over z, y), rows: 4 (over x, core).
Axes of the slice: x: 2, y: 2, z: 4, core: 2. Of those that a mesh axis runs over, the one named last changes fastest.
Arguments:
- master_down: float32 [16, 6400, 4096], P('owner', None, 'rows'), may hold values from -0.109375 to 0.109375
- router_weight: float32 [4096, 16], P('rows', 'owner'), may hold values from -0.09375 to 0.09375
- router_gain: float32 [4096], P('rows'), may hold values from 0.25 to 1.75
Outputs:
- final_down: bfloat16 [16, 6400, 4096], P('owner', 'rows')
- scale_down: float32 [16, 6400], P('owner', 'rows')
- serve_router: bfloat16 [4096, 16], replicated
All inputs are finite; a program needn't handle non-finite values. Where the computation divides by a largest or mean magnitude, that divisor is 1e-20 or more.
Results may differ from a plain program's by a relative error of at most 0.001.
Values may be sent and summed in bfloat16 or wider, within the bound.
A program may use at most 192 MiB of HBM per device.

v0:
```python
import jax
import jax.numpy as jnp
from jax import lax
from jax.sharding import PartitionSpec as P

D_MODEL = 4096


def per_device(master_down, router_weight, router_gain):
    total_down = lax.psum(jnp.sum(jnp.abs(master_down), axis=2), "rows")
    scale_down = total_down / D_MODEL
    narrow_down = (master_down / jnp.expand_dims(scale_down, 2)).astype(jnp.bfloat16)
    final_down = lax.all_to_all(narrow_down, "rows", split_axis=1, concat_axis=2, tiled=True)
    scale_down = lax.dynamic_slice_in_dim(
        scale_down, lax.axis_index("rows") * final_down.shape[1], final_down.shape[1], axis=1
    )
    part_router = (router_weight * router_gain[:, None]).astype(jnp.bfloat16)
    row_router = lax.all_gather(part_router, "rows", axis=0, tiled=True)
    serve_router = lax.all_gather(row_router, "owner", axis=1, tiled=True)
    return (final_down, scale_down, serve_router)


def solution(mesh):
    return jax.shard_map(
        per_device,
        mesh=mesh,
        in_specs=(P("owner", None, "rows"), P("rows", "owner"), P("rows")),
        out_specs=(P("owner", "rows", None), P("owner", "rows"), P()),
        check_vma=False,
    )
```

profile of v0, /device:TPU:0, one launch (start us, length us, event | category | flops | bytes accessed | tf_op | source)
XLA Modules:
  0.0 506.3 jit_solution(15090514093543817720)
XLA Ops:
  0.6 17.0 %abs_reduce_fusion = f32[2,6400]{1,0:T(2,128)S(1)} fusion(f32[2,6400,1024]{2,1,0:T(8,128)} %param.3), kind=kLoop, calls=%fused_computation.1 | loop fusion | flops 26201600 | bytes 52480000 | tf_op jit(solution)/shard_map/reduce_sum | solution.py:10
  17.6 13.4 %psum.7 = f32[2,6400]{1,0:T(2,128)S(1)} all-reduce(f32[2,6400]{1,0:T(2,128)S(1)} %abs_reduce_fusion), channel_id=1, replica_groups=mesh['owner'=8,'rows'=4] {'rows'}, use_global_device_ids=true, to_apply=%region_1.0 | all-reduce | flops 12800 | bytes 102400 | tf_op jit(solution)/shard_map/psum | solution.py:10
  31.1 26.1 %divide_convert_fusion = bf16[2,6400,1024]{2,1,0:T(8,128)(2,1)} fusion(f32[2,6400,1024]{2,1,0:T(8,128)} %param.3, f32[2,6400]{1,0:T(2,128)S(1)} %broadcast_multiply_fusion), kind=kLoop, calls=%fused_computation | loop fusion | flops 26214400 | bytes 78694400 | tf_op jit(solution)/shard_map/convert_element_type | solution.py:12
  57.2 0.0 copy-start
  57.2 0.0 copy-start.1
  57.2 47.4 %copy.10 = bf16[2,6400,1024]{2,0,1:T(2,128)(2,1)} copy(bf16[2,6400,1024]{2,1,0:T(8,128)(2,1)} %divide_convert_fusion) | data formatting | bytes 52428800 | tf_op jit(solution)/shard_map/convert_element_type | solution.py:12
  104.6 8.6 %all-to-all-start = ((bf16[2,6400,1024]{2,0,1:T(2,128)(2,1)}), bf16[2,6400,1024]{2,0,1:T(2,128)(2,1)}, u32[]{:S(2)}, u32[]{:S(2)}) async-start(bf16[2,6400,1024]{2,0,1:T(2,128)(2,1)} %copy.10), calls=%async_computation | async-start | bytes 52428800 | tf_op jit(solution)/shard_map/all_to_all | solution.py:13
  113.2 0.0 copy-done
  113.2 0.0 copy-done.1
  113.2 285.0 %all_gather.6 = bf16[4096,2]{0,1:T(2,128)(2,1)S(1)} all-gather(bf16[1024,2]{0,1:T(2,128)(2,1)S(1)} %multiply_convert_fusion), channel_id=1, replica_groups=mesh['owner'=8,'rows'=4] {'rows'}, dimensions={0}, use_global_device_ids=true | all-gather | bytes 20480 | tf_op jit(solution)/shard_map/all_gather | solution.py:18
  398.2 30.9 %all-gather = bf16[8,2,4096]{2,1,0:T(2,128)(2,1)S(1)} all-gather(bf16[1,2,4096]{2,1,0:T(2,128)(2,1)S(1)} %bitcast.8), channel_id=1, replica_groups=mesh['owner'=8,'rows'=4] {'owner'}, dimensions={0}, use_global_device_ids=true | all-gather | bytes 147456 | tf_op jit(solution)/shard_map/all_gather | solution.py:19
  429.1 0.7 reshape.9
  429.8 0.7 constant_dynamic-slice_fusion
  430.5 0.0 all-to-all-done
  430.5 33.4 %copy.11 = bf16[2,1600,4,1024]{3,2,1,0:T(4,128)(2,1)} copy(bf16[2,1600,4,1024]{3,0,1,2:T(2,128)(2,1)} %bitcast.1) | data formatting | bytes 52428800 | tf_op jit(solution)/shard_map/all_to_all | solution.py:13
  463.9 42.5 %all_to_all.16 = bf16[2,1600,4096]{2,1,0:T(8,128)(2,1)} reshape(bf16[2,1600,4,1024]{3,2,1,0:T(4,128)(2,1)} %copy.11) | data formatting | bytes 52428800 | tf_op jit(solution)/shard_map/all_to_all | solution.py:13
  (2 shorter events, 0.0 us)
Async XLA Ops:
  57.2 56.0 %copy-start = (f32[1024,2]{0,1:T(2,128)S(1)}, f32[1024,2]{0,1:T(2,128)}, u32[]{:S(2)}) copy-start(f32[1024,2]{0,1:T(2,128)} %param.4) | copy-start | bytes 24580
  57.2 56.0 %copy-start.1 = (f32[1024]{0:T(1024)S(1)}, f32[1024]{0:T(1024)}, u32[]{:S(2)}) copy-start(f32[1024]{0:T(1024)} %param.5) | copy-start | bytes 12292
  104.6 325.9 %all-to-all-start = ((bf16[2,6400,1024]{2,0,1:T(2,128)(2,1)}), bf16[2,6400,1024]{2,0,1:T(2,128)(2,1)}, u32[]{:S(2)}, u32[]{:S(2)}) async-start(bf16[2,6400,1024]{2,0,1:T(2,128)(2,1)} %copy.10), calls=%async_computation | async-start | bytes 52428800 | tf_op jit(solution)/shard_map/all_to_all | solution.py:13
where the time goes:
time: 508 us; the launch traced here: 506 us
  blocking collectives  329 us (65%)
  local copies, waits for them, and re-layouts  125 us (25%)
  other arithmetic  43.2 us (9%)
  starting transfers between devices  8.59 us (2%)
    all_gather x1, blocking collectives, per_device(): row_router = lax.all_gather(part_router, 'rows', axis=0, tiled=True)  285 us
    all_to_all x2, local copies, waits for them, and re-layouts, per_device(): lax.all_to_all(narrow_down, 'rows', split_axis=1, concat_axis=2, tiled=True)  75.8 us
    convert_element_type x1, local copies, waits for them, and re-layouts, per_device(): (master_down / jnp.expand_dims(scale_down, 2)).astype(jnp.bfloat16)  47.4 us
    all_gather x1, blocking collectives, per_device(): serve_router = lax.all_gather(row_router, 'owner', axis=1, tiled=True)  30.9 us
    convert_element_type x1, other arithmetic, per_device(): (master_down / jnp.expand_dims(scale_down, 2)).astype(jnp.bfloat16)  26.1 us
    reduce_sum x1, other arithmetic, per_device(): total_down = lax.psum(jnp.sum(jnp.abs(master_down), axis=2), 'rows')  17 us
    psum x1, blocking collectives, per_device(): total_down = lax.psum(jnp.sum(jnp.abs(master_down), axis=2), 'rows')  13.4 us
  transfers between devices with their start and end apart: 1, of which 0 were waited for; matrix products, arithmetic and copies ran while one was open for 0% of the time, Pallas kernels for 0%

commit v1 on v0

--- a/solution.py
+++ b/solution.py
@@ -16,7 +16,7 @@
     )
     part_router = (router_weight * router_gain[:, None]).astype(jnp.bfloat16)
     row_router = lax.all_gather(part_router, "rows", axis=0, tiled=True)
-    serve_router = lax.all_gather(row_router, "owner", axis=1, tiled=True)
+    serve_router = jnp.concatenate(lax.all_gather(row_router, axis_name="owner"), axis=1)
     return (final_down, scale_down, serve_router)
 
 

time: 508 us -> 508 us (level)
  no operation moved by 1% of the time
where the time goes in v1:
time: 508 us; the launch traced here: 506 us
  blocking collectives  329 us (65%)
  local copies, waits for them, and re-layouts  125 us (25%)
  other arithmetic  43.2 us (9%)
  starting transfers between devices  8.59 us (2%)
    all_gather x1, blocking collectives, per_device(): row_router = lax.all_gather(part_router, 'rows', axis=0, tiled=True)  285 us
    all_to_all x2, local copies, waits for them, and re-layouts, per_device(): lax.all_to_all(narrow_down, 'rows', split_axis=1, concat_axis=2, tiled=True)  75.8 us
    convert_element_type x1, local copies, waits for them, and re-layouts, per_device(): (master_down / jnp.expand_dims(scale_down, 2)).astype(jnp.bfloat16)  47.4 us
    all_gather x1, blocking collectives, per_device(): lax.all_gather(row_router, axis_name='owner')  30.9 us
    convert_element_type x1, other arithmetic, per_device(): (master_down / jnp.expand_dims(scale_down, 2)).astype(jnp.bfloat16)  26.1 us
    reduce_sum x1, other arithmetic, per_device(): total_down = lax.psum(jnp.sum(jnp.abs(master_down), axis=2), 'rows')  17 us
    psum x1, blocking collectives, per_device(): total_down = lax.psum(jnp.sum(jnp.abs(master_down), axis=2), 'rows')  13.4 us
  transfers between devices with their start and end apart: 1, of which 0 were waited for; matrix products, arithmetic and copies ran while one was open for 0% of the time, Pallas kernels for 0%

profile of v1, /device:TPU:0, one launch (start us, length us, event | category | flops | bytes accessed | tf_op | source)
XLA Modules:
  0.0 506.3 jit_solution(16051430214802116243)
XLA Ops:
  0.6 17.0 %abs_reduce_fusion = f32[2,6400]{1,0:T(2,128)S(1)} fusion(f32[2,6400,1024]{2,1,0:T(8,128)} %param.3), kind=kLoop, calls=%fused_computation.1 | loop fusion | flops 26201600 | bytes 52480000 | tf_op jit(solution)/shard_map/reduce_sum | solution.py:10
  17.6 13.4 %psum.7 = f32[2,6400]{1,0:T(2,128)S(1)} all-reduce(f32[2,6400]{1,0:T(2,128)S(1)} %abs_reduce_fusion), channel_id=1, replica_groups=mesh['owner'=8,'rows'=4] {'rows'}, use_global_device_ids=true, to_apply=%region_1.0 | all-reduce | flops 12800 | bytes 102400 | tf_op jit(solution)/shard_map/psum | solution.py:10
  31.1 26.1 %divide_convert_fusion = bf16[2,6400,1024]{2,1,0:T(8,128)(2,1)} fusion(f32[2,6400,1024]{2,1,0:T(8,128)} %param.3, f32[2,6400]{1,0:T(2,128)S(1)} %broadcast_multiply_fusion), kind=kLoop, calls=%fused_computation | loop fusion | flops 26214400 | bytes 78694400 | tf_op jit(solution)/shard_map/convert_element_type | solution.py:12
  57.2 0.0 copy-start
  57.2 0.0 copy-start.1
  57.2 47.4 %copy.12 = bf16[2,6400,1024]{2,0,1:T(2,128)(2,1)} copy(bf16[2,6400,1024]{2,1,0:T(8,128)(2,1)} %divide_convert_fusion) | data formatting | bytes 52428800 | tf_op jit(solution)/shard_map/convert_element_type | solution.py:12
  104.6 8.6 %all-to-all-start = ((bf16[2,6400,1024]{2,0,1:T(2,128)(2,1)}), bf16[2,6400,1024]{2,0,1:T(2,128)(2,1)}, u32[]{:S(2)}, u32[]{:S(2)}) async-start(bf16[2,6400,1024]{2,0,1:T(2,128)(2,1)} %copy.12), calls=%async_computation | async-start | bytes 52428800 | tf_op jit(solution)/shard_map/all_to_all | solution.py:13
  113.2 0.0 copy-done
  113.2 0.0 copy-done.1
  113.2 285.0 %all_gather.9 = bf16[4096,2]{0,1:T(2,128)(2,1)S(1)} all-gather(bf16[1024,2]{0,1:T(2,128)(2,1)S(1)} %multiply_convert_fusion), channel_id=1, replica_groups=mesh['owner'=8,'rows'=4] {'rows'}, dimensions={0}, use_global_device_ids=true | all-gather | bytes 20480 | tf_op jit(solution)/shard_map/all_gather | solution.py:18
  398.2 30.9 %all-gather = bf16[32768,2]{0,1:T(2,128)(2,1)S(1)} all-gather(bf16[4096,2]{0,1:T(2,128)(2,1)S(1)} %all_gather.9), channel_id=2, replica_groups=mesh['owner'=8,'rows'=4] {'owner'}, dimensions={0}, use_global_device_ids=true | all-gather | bytes 147456 | tf_op jit(solution)/shard_map/all_gather | solution.py:19
  429.1 0.7 reshape.15
  429.8 0.7 constant_dynamic-slice_fusion
  430.5 0.0 all-to-all-done
  430.5 33.4 %copy.13 = bf16[2,1600,4,1024]{3,2,1,0:T(4,128)(2,1)} copy(bf16[2,1600,4,1024]{3,0,1,2:T(2,128)(2,1)} %bitcast.1) | data formatting | bytes 52428800 | tf_op jit(solution)/shard_map/all_to_all | solution.py:13
  463.9 42.5 %all_to_all.16 = bf16[2,1600,4096]{2,1,0:T(8,128)(2,1)} reshape(bf16[2,1600,4,1024]{3,2,1,0:T(4,128)(2,1)} %copy.13) | data formatting | bytes 52428800 | tf_op jit(solution)/shard_map/all_to_all | solution.py:13
  (2 shorter events, 0.0 us)
Async XLA Ops:
  57.2 56.0 %copy-start = (f32[1024,2]{0,1:T(2,128)S(1)}, f32[1024,2]{0,1:T(2,128)}, u32[]{:S(2)}) copy-start(f32[1024,2]{0,1:T(2,128)} %param.4) | copy-start | bytes 24580
  57.2 56.0 %copy-start.1 = (f32[1024]{0:T(1024)S(1)}, f32[1024]{0:T(1024)}, u32[]{:S(2)}) copy-start(f32[1024]{0:T(1024)} %param.5) | copy-start | bytes 12292
  104.6 325.9 %all-to-all-start = ((bf16[2,6400,1024]{2,0,1:T(2,128)(2,1)}), bf16[2,6400,1024]{2,0,1:T(2,128)(2,1)}, u32[]{:S(2)}, u32[]{:S(2)}) async-start(bf16[2,6400,1024]{2,0,1:T(2,128)(2,1)} %copy.12), calls=%async_computation | async-start | bytes 52428800 | tf_op jit(solution)/shard_map/all_to_all | solution.py:13
